TPU v7x, 256 devices: a whole 4x4x8 slice. The times are simulated.
256 devices in a mesh: expert: 8 (over x, core), shard: 32 (over z, y).
Axes of the slice: x: 4, y: 4, z: 8, core: 2. Of those that a mesh axis runs over, the one named last changes fastest.
Arguments:
- train_down: float32 [16, 6400, 4096], P('expert', None, 'shard'), may hold values from -0.15625 to 0.15625
- other_down: bfloat16 [16, 6400, 4096], P('expert', None, 'shard'), may hold values from -0.0390625 to 0.0390625
- router_weight: float32 [4096, 16], P('shard', 'expert'), may hold values from -0.09375 to 0.09375
- router_gain: float32 [4096], P('shard'), may hold values from 0.25 to 1.75
Outputs:
- ready_down: bfloat16 [16, 6400, 4096], P('expert', 'shard')
- scale_down: float32 [16, 6400], P('expert', 'shard')
- serve_router: bfloat16 [4096, 16], replicated
All inputs are finite; a program needn't handle non-finite values. Where the computation divides by a largest or mean magnitude, that divisor is 1e-20 or more.
Results may differ from a plain program's by a relative error of at most 0.001.
Values may be sent and summed in bfloat16 or wider, within the bound.
A program may use at most 64 MiB of HBM per device.

v0:
```python
import jax
import jax.numpy as jnp
from jax import lax
from jax.sharding import PartitionSpec as P


def sent_to_all(x, axis):
    copies = jnp.broadcast_to(x, (lax.axis_size(axis), *x.shape))
    return lax.all_to_all(copies, axis, split_axis=0, concat_axis=0, tiled=True)


def of_everyone(x, axis):
    everything = sent_to_all(x, axis)
    return jnp.max(everything, axis=0)


def laid_out(parts, dim):
    lengths = list(parts.shape[1:])
    lengths[dim] *= parts.shape[0]
    return jnp.moveaxis(parts, 0, dim).reshape(lengths)


def gathered_copies(x, axis, dim):
    return laid_out(sent_to_all(x, axis), dim)


def per_device(train_down, other_down, router_weight, router_gain):
    latest_down = train_down + other_down.astype(jnp.float32)
    scale_down = of_everyone(jnp.max(jnp.abs(latest_down), axis=2), "shard")
    narrow_down = (latest_down / jnp.expand_dims(scale_down, 2)).astype(jnp.bfloat16)
    ready_down = lax.all_to_all(narrow_down, "shard", split_axis=1, concat_axis=2, tiled=True)
    scale_down = lax.dynamic_slice_in_dim(
        scale_down, lax.axis_index("shard") * ready_down.shape[1], ready_down.shape[1], axis=1
    )
    part_router = (router_weight * router_gain[:, None]).astype(jnp.bfloat16)
    row_router = gathered_copies(part_router, "shard", 0)
    serve_router = gathered_copies(row_router, "expert", 1)
    return (ready_down, scale_down, serve_router)


def solution(mesh):
    in_specs = (
        P("expert", None, "shard"),
        P("expert", None, "shard"),
        P("shard", "expert"),
        P("shard"),
    )
    out_specs = (P("expert", "shard", None), P("expert", "shard"), P())
    return jax.shard_map(
        per_device, mesh=mesh, in_specs=in_specs, out_specs=out_specs, check_vma=False
    )
```

profile of v0, /device:TPU:9, one launch (start us, length us, event | category | flops | bytes accessed | tf_op | source)
XLA Modules:
  0.0 201.1 jit_solution(1283728771421727400)
XLA Ops:
  0.6 0.7 multiply_convert_fusion
  1.3 0.6 broadcast_in_dim.12
  1.9 11.1 %all-to-all-start.2 = ((bf16[32,128,2]{1,2,0:T(2,128)(2,1)}), bf16[32,128,2]{1,2,0:T(2,128)(2,1)S(1)}, u32[]{:S(2)}, u32[]{:S(2)}) async-start(bf16[32,128,2]{1,2,0:T(2,128)(2,1)} %broadcast_in_dim.12), calls=%async_computation.2 | async-start | bytes 32768 | tf_op jit(solution)/shard_map/all_to_all | solution.py:9
  13.1 5.6 %abs_reduce_fusion = f32[2,6400]{1,0:T(2,128)S(1)} fusion(f32[2,6400,128]{2,1,0:T(8,128)} %param.4, bf16[2,6400,128]{2,1,0:T(8,128)(2,1)} %param.5), kind=kLoop, calls=%fused_computation.1 | loop fusion | flops 6540800 | bytes 9881600 | tf_op jit(solution)/shard_map/reduce_max | solution.py:29
  18.7 0.0 copy-start
  18.7 2.0 all-to-all-done.2
  20.7 0.4 broadcast_in_dim.11
  21.1 46.8 %all_to_all.33 = f32[32,2,6400]{2,1,0:T(2,128)} all-to-all(f32[32,2,6400]{2,1,0:T(2,128)S(1)} %broadcast_in_dim.11), channel_id=1, replica_groups=mesh['expert'=8,'shard'=32] {'shard'}, dimensions={0} | all-to-all | bytes 3276800 | tf_op jit(solution)/shard_map/all_to_all | solution.py:9
  67.9 0.7 broadcast_in_dim.13
  68.6 6.7 %all-to-all-start.3 = ((bf16[8,4096,2]{1,2,0:T(2,128)(2,1)}), bf16[8,4096,2]{1,2,0:T(2,128)(2,1)S(1)}, u32[]{:S(2)}, u32[]{:S(2)}) async-start(bf16[8,4096,2]{1,2,0:T(2,128)(2,1)} %broadcast_in_dim.13), calls=%async_computation.3 | async-start | bytes 262144 | tf_op jit(solution)/shard_map/all_to_all | solution.py:9
  75.4 1.9 reduce_max.19
  77.3 0.0 copy-done
  77.3 4.7 %divide_convert_fusion = bf16[2,6400,128]{2,1,0:T(8,128)(2,1)S(1)} fusion(f32[2,6400,128]{2,1,0:T(8,128)} %param.4, bf16[2,6400,128]{2,1,0:T(8,128)(2,1)S(1)} %copy-done, f32[2,6400]{1,0:T(2,128)S(1)} %reduce_max.19), kind=kLoop, calls=%fused_computation | loop fusion | flops 6553600 | bytes 13158400 | tf_op jit(solution)/shard_map/convert_element_type | solution.py:30
  82.0 27.9 %copy.31 = bf16[2,6400,128]{2,0,1:T(2,128)(2,1)} copy(bf16[2,6400,128]{2,1,0:T(8,128)(2,1)S(1)} %divide_convert_fusion) | data formatting | bytes 6553600 | tf_op jit(solution)/shard_map/convert_element_type | solution.py:30
  109.9 0.0 all-to-all-done.3
  109.9 5.0 %all-to-all-start.1 = ((bf16[2,6400,128]{2,0,1:T(2,128)(2,1)}), bf16[2,6400,128]{2,0,1:T(2,128)(2,1)S(1)}, u32[]{:S(2)}, u32[]{:S(2)}) async-start(bf16[2,6400,128]{2,0,1:T(2,128)(2,1)} %copy.31), calls=%async_computation.1 | async-start | bytes 6553600 | tf_op jit(solution)/shard_map/all_to_all | solution.py:31
  114.9 0.7 reshape.15
  115.6 0.7 constant_dynamic-slice_fusion
  116.3 76.1 %all-to-all-done.1 = bf16[2,6400,128]{2,0,1:T(2,128)(2,1)S(1)} async-done(((bf16[2,6400,128]{2,0,1:T(2,128)(2,1)}), bf16[2,6400,128]{2,0,1:T(2,128)(2,1)S(1)}, u32[]{:S(2)}, u32[]{:S(2)}) %all-to-all-start.1) | async-done | bytes 3276832 | tf_op jit(solution)/shard_map/all_to_all | solution.py:31
  192.4 2.5 %copy.32 = bf16[2,200,32,128]{3,2,1,0:T(8,128)(2,1)} copy(bf16[2,200,32,128]{3,0,1,2:T(2,128)(2,1)S(1)} %bitcast.9) | data formatting | bytes 6553600 | tf_op jit(solution)/shard_map/all_to_all | solution.py:31
  194.9 6.2 %all_to_all.26 = bf16[2,200,4096]{2,1,0:T(8,128)(2,1)} reshape(bf16[2,200,32,128]{3,2,1,0:T(8,128)(2,1)} %copy.32) | data formatting | bytes 6553600 | tf_op jit(solution)/shard_map/all_to_all | solution.py:31
Async XLA Ops:
  1.9 18.8 %all-to-all-start.2 = ((bf16[32,128,2]{1,2,0:T(2,128)(2,1)}), bf16[32,128,2]{1,2,0:T(2,128)(2,1)S(1)}, u32[]{:S(2)}, u32[]{:S(2)}) async-start(bf16[32,128,2]{1,2,0:T(2,128)(2,1)} %broadcast_in_dim.12), calls=%async_computation.2 | async-start | bytes 32768 | tf_op jit(solution)/shard_map/all_to_all | solution.py:9
  18.7 58.6 %copy-start = (bf16[2,6400,128]{2,1,0:T(8,128)(2,1)S(1)}, bf16[2,6400,128]{2,1,0:T(8,128)(2,1)}, u32[]{:S(2)}) copy-start(bf16[2,6400,128]{2,1,0:T(8,128)(2,1)} %param.5) | copy-start | bytes 9830404
  68.6 41.3 %all-to-all-start.3 = ((bf16[8,4096,2]{1,2,0:T(2,128)(2,1)}), bf16[8,4096,2]{1,2,0:T(2,128)(2,1)S(1)}, u32[]{:S(2)}, u32[]{:S(2)}) async-start(bf16[8,4096,2]{1,2,0:T(2,128)(2,1)} %broadcast_in_dim.13), calls=%async_computation.3 | async-start | bytes 262144 | tf_op jit(solution)/shard_map/all_to_all | solution.py:9
  109.9 82.5 %all-to-all-start.1 = ((bf16[2,6400,128]{2,0,1:T(2,128)(2,1)}), bf16[2,6400,128]{2,0,1:T(2,128)(2,1)S(1)}, u32[]{:S(2)}, u32[]{:S(2)}) async-start(bf16[2,6400,128]{2,0,1:T(2,128)(2,1)} %copy.31), calls=%async_computation.1 | async-start | bytes 6553600 | tf_op jit(solution)/shard_map/all_to_all | solution.py:31
where the time goes:
time: 202 us; the launch traced here: 201 us
  waiting for transfers between devices  78.1 us (39%)
  blocking collectives  46.8 us (23%)
  local copies, waits for them, and re-layouts  39.7 us (20%)
  starting transfers between devices  22.9 us (11%)
  other arithmetic  12.9 us (6%)
    all_to_all x1, waiting for transfers between devices, per_device(): lax.all_to_all(narrow_down, 'shard', split_axis=1, concat_axis=2, tiled=T...  76.1 us
    all_to_all x1, blocking collectives, sent_to_all(): return lax.all_to_all(copies, axis, split_axis=0, concat_axis=0, tiled=True)  46.8 us
    convert_element_type x1, local copies, waits for them, and re-layouts, per_device(): (latest_down / jnp.expand_dims(scale_down, 2)).astype(jnp.bfloat16)  27.9 us
    all_to_all x2, starting transfers between devices, sent_to_all(): return lax.all_to_all(copies, axis, split_axis=0, concat_axis=0, tiled=True)  17.8 us
    all_to_all x2, local copies, waits for them, and re-layouts, per_device(): lax.all_to_all(narrow_down, 'shard', split_axis=1, concat_axis=2, tiled=T...  8.72 us
    reduce_max x1, other arithmetic, per_device(): scale_down = of_everyone(jnp.max(jnp.abs(latest_down), axis=2), 'shard')  5.6 us
    all_to_all x1, starting transfers between devices, per_device(): lax.all_to_all(narrow_down, 'shard', split_axis=1, concat_axis=2, tiled=T...  5.01 us
    convert_element_type x1, other arithmetic, per_device(): (latest_down / jnp.expand_dims(scale_down, 2)).astype(jnp.bfloat16)  4.74 us
  transfers between devices with their start and end apart: 3, of which 2 were waited for; matrix products, arithmetic and copies ran while one was open for 21% of the time, Pallas kernels for 0%

commit v1 on v0

--- a/solution.py
+++ b/solution.py
@@ -2,6 +2,12 @@
 import jax.numpy as jnp
 from jax import lax
 from jax.sharding import PartitionSpec as P
+
+
+def swap_blocks(x, axis, split, join):
+    parts = jnp.split(x, lax.axis_size(axis), axis=split)
+    received = lax.all_to_all(jnp.stack(parts), axis, 0, 0)
+    return jnp.concatenate(received, axis=join)
 
 
 def sent_to_all(x, axis):
@@ -28,7 +34,7 @@
     latest_down = train_down + other_down.astype(jnp.float32)
     scale_down = of_everyone(jnp.max(jnp.abs(latest_down), axis=2), "shard")
     narrow_down = (latest_down / jnp.expand_dims(scale_down, 2)).astype(jnp.bfloat16)
-    ready_down = lax.all_to_all(narrow_down, "shard", split_axis=1, concat_axis=2, tiled=True)
+    ready_down = swap_blocks(narrow_down, "shard", 1, 2)
     scale_down = lax.dynamic_slice_in_dim(
         scale_down, lax.axis_index("shard") * ready_down.shape[1], ready_down.shape[1], axis=1
     )

time: 202 us -> 169 us (0.84)
  local copies, waits for them, and re-layouts: 39.7 us -> 7.53 us
    convert_element_type x1 -> x0, local copies, waits for them, and re-layouts: 27.9 us -> none  [per_device(): (latest_down / jnp.expand_dims(scale_down, 2)).astype(jnp.bfloat16)]
    all_to_all x2 -> x0, local copies, waits for them, and re-layouts: 8.72 us -> none  [per_device(): lax.all_to_all(narrow_down, 'shard', split_axis=1, concat_axis=2, tiled=T...]
    unnamed x2 -> x35, local copies, waits for them, and re-layouts: 0.01 us -> 2.25 us
    reshape x0 -> x1, local copies, waits for them, and re-layouts: none -> 2.14 us  [swap_blocks(): return jnp.concatenate(received, axis=join)]
  transfers between devices with their start and end apart: 3 -> 3, of which waited for: 2 -> 2; matrix products, arithmetic and copies ran while one was open for 21% -> 8% of each run, Pallas kernels for 0% -> 0%
where the time goes in v1:
time: 169 us
  waiting for transfers between devices  78.1 us (46%)
  blocking collectives  46.8 us (28%)
  starting transfers between devices  22.9 us (14%)
  other arithmetic  12.9 us (8%)
  local copies, waits for them, and re-layouts  7.53 us (4%)
    all_to_all x1, waiting for transfers between devices, swap_blocks(): received = lax.all_to_all(jnp.stack(parts), axis, 0, 0)  76.1 us
    all_to_all x1, blocking collectives, sent_to_all(): return lax.all_to_all(copies, axis, split_axis=0, concat_axis=0, tiled=True)  46.8 us
    all_to_all x2, starting transfers between devices, sent_to_all(): return lax.all_to_all(copies, axis, split_axis=0, concat_axis=0, tiled=True)  17.8 us
    reduce_max x1, other arithmetic, per_device(): scale_down = of_everyone(jnp.max(jnp.abs(latest_down), axis=2), 'shard')  5.6 us
    all_to_all x1, starting transfers between devices, swap_blocks(): received = lax.all_to_all(jnp.stack(parts), axis, 0, 0)  5.01 us
    convert_element_type x1, other arithmetic, per_device(): (latest_down / jnp.expand_dims(scale_down, 2)).astype(jnp.bfloat16)  4.74 us
  transfers between devices with their start and end apart: 3, of which 2 were waited for; matrix products, arithmetic and copies ran while one was open for 8% of the time, Pallas kernels for 0%

profile of v1, /device:TPU:9, one launch (start us, length us, event | category | flops | bytes accessed | tf_op | source)
XLA Modules:
  0.0 169.1 jit_solution(7231324775538372856)
XLA Ops:
  0.6 0.7 multiply_convert_fusion
  1.3 0.6 broadcast_in_dim.12
  1.9 11.1 %all-to-all-start.2 = ((bf16[32,128,2]{1,2,0:T(2,128)(2,1)}), bf16[32,128,2]{1,2,0:T(2,128)(2,1)S(1)}, u32[]{:S(2)}, u32[]{:S(2)}) async-start(bf16[32,128,2]{1,2,0:T(2,128)(2,1)} %broadcast_in_dim.12), calls=%async_computation.2 | async-start | bytes 32768 | tf_op jit(solution)/shard_map/all_to_all | solution.py:15
  13.1 5.6 %abs_reduce_fusion = f32[2,6400]{1,0:T(2,128)S(1)} fusion(f32[2,6400,128]{2,1,0:T(8,128)} %param.4, bf16[2,6400,128]{2,1,0:T(8,128)(2,1)} %param.5), kind=kLoop, calls=%fused_computation.1 | loop fusion | flops 6540800 | bytes 9881600 | tf_op jit(solution)/shard_map/reduce_max | solution.py:35
  18.7 0.0 copy-start
  18.7 2.0 %all-to-all-done.2 = bf16[32,128,2]{1,2,0:T(2,128)(2,1)S(1)} async-done(((bf16[32,128,2]{1,2,0:T(2,128)(2,1)}), bf16[32,128,2]{1,2,0:T(2,128)(2,1)S(1)}, u32[]{:S(2)}, u32[]{:S(2)}) %all-to-all-start.2) | async-done | bytes 16416 | tf_op jit(solution)/shard_map/all_to_all | solution.py:15
  20.7 0.4 broadcast_in_dim.11
  21.1 46.8 %all_to_all.20 = f32[32,2,6400]{2,1,0:T(2,128)} all-to-all(f32[32,2,6400]{2,1,0:T(2,128)S(1)} %broadcast_in_dim.11), channel_id=1, replica_groups=mesh['expert'=8,'shard'=32] {'shard'}, dimensions={0} | all-to-all | bytes 3276800 | tf_op jit(solution)/shard_map/all_to_all | solution.py:15
  67.9 0.7 broadcast_in_dim.13
  68.6 6.7 %all-to-all-start.3 = ((bf16[8,4096,2]{1,2,0:T(2,128)(2,1)}), bf16[8,4096,2]{1,2,0:T(2,128)(2,1)S(1)}, u32[]{:S(2)}, u32[]{:S(2)}) async-start(bf16[8,4096,2]{1,2,0:T(2,128)(2,1)} %broadcast_in_dim.13), calls=%async_computation.3 | async-start | bytes 262144 | tf_op jit(solution)/shard_map/all_to_all | solution.py:15
  75.4 1.9 %reduce_max.19 = f32[2,6400]{1,0:T(2,128)S(1)} reduce(f32[32,2,6400]{2,1,0:T(2,128)} %all_to_all.20, f32[]{:T(128)} %constant.5.clone.1), dimensions={0}, to_apply=%region_1.0 | reduce | flops 396800 | bytes 1689604 | tf_op jit(solution)/shard_map/reduce_max | solution.py:20
  77.3 0.0 copy-done
  77.3 4.7 %divide_convert_fusion = bf16[2,6400,128]{2,1,0:T(8,128)(2,1)S(1)} fusion(f32[2,6400,128]{2,1,0:T(8,128)} %param.4, bf16[2,6400,128]{2,1,0:T(8,128)(2,1)S(1)} %copy-done, f32[2,6400]{1,0:T(2,128)S(1)} %reduce_max.19), kind=kLoop, calls=%fused_computation | loop fusion | flops 6553600 | bytes 13158400 | tf_op jit(solution)/shard_map/convert_element_type | solution.py:36
  82.8 0.0 copy-start.1
  82.8 1.7 %copy-done.1 = bf16[32,2,200,128]{3,2,1,0:T(8,128)(2,1)} copy-done((bf16[32,2,200,128]{3,2,1,0:T(8,128)(2,1)}, bf16[32,2,200,128]{3,2,1,0:T(8,128)(2,1)S(1)}, u32[]{:S(2)}) %copy-start.1) | copy-done | bytes 3276824
  84.5 0.0 all-to-all-done.3
  84.5 5.0 %all-to-all-start.1 = ((bf16[32,2,200,128]{3,2,1,0:T(8,128)(2,1)}), bf16[32,2,200,128]{3,2,1,0:T(8,128)(2,1)S(1)}, u32[]{:S(2)}, u32[]{:S(2)}) async-start(bf16[32,2,200,128]{3,2,1,0:T(8,128)(2,1)} %copy-done.1), calls=%async_computation.1 | async-start | bytes 6553600 | tf_op jit(solution)/shard_map/all_to_all | solution.py:9
  89.5 0.7 reshape.23
  90.2 0.7 constant_dynamic-slice_fusion
  90.9 76.1 %all-to-all-done.1 = bf16[32,2,200,128]{3,2,1,0:T(8,128)(2,1)S(1)} async-done(((bf16[32,2,200,128]{3,2,1,0:T(8,128)(2,1)}), bf16[32,2,200,128]{3,2,1,0:T(8,128)(2,1)S(1)}, u32[]{:S(2)}, u32[]{:S(2)}) %all-to-all-start.1) | async-done | bytes 3276832 | tf_op jit(solution)/shard_map/all_to_all | solution.py:9
  167.0 2.1 %copy_bitcast_fusion = bf16[2,200,4096]{2,1,0:T(8,128)(2,1)} fusion(bf16[32,2,200,128]{3,2,1,0:T(8,128)(2,1)S(1)} %all-to-all-done.1), kind=kLoop, calls=%fused_computation.3 | loop fusion | bytes 6553600 | tf_op jit(solution)/shard_map/reshape | solution.py:10
  (32 shorter events, 0.6 us)
Async XLA Ops:
  1.9 18.8 %all-to-all-start.2 = ((bf16[32,128,2]{1,2,0:T(2,128)(2,1)}), bf16[32,128,2]{1,2,0:T(2,128)(2,1)S(1)}, u32[]{:S(2)}, u32[]{:S(2)}) async-start(bf16[32,128,2]{1,2,0:T(2,128)(2,1)} %broadcast_in_dim.12), calls=%async_computation.2 | async-start | bytes 32768 | tf_op jit(solution)/shard_map/all_to_all | solution.py:15
  18.7 58.6 %copy-start = (bf16[2,6400,128]{2,1,0:T(8,128)(2,1)S(1)}, bf16[2,6400,128]{2,1,0:T(8,128)(2,1)}, u32[]{:S(2)}) copy-start(bf16[2,6400,128]{2,1,0:T(8,128)(2,1)} %param.5) | copy-start | bytes 9830404
  68.6 15.9 %all-to-all-start.3 = ((bf16[8,4096,2]{1,2,0:T(2,128)(2,1)}), bf16[8,4096,2]{1,2,0:T(2,128)(2,1)S(1)}, u32[]{:S(2)}, u32[]{:S(2)}) async-start(bf16[8,4096,2]{1,2,0:T(2,128)(2,1)} %broadcast_in_dim.13), calls=%async_computation.3 | async-start | bytes 262144 | tf_op jit(solution)/shard_map/all_to_all | solution.py:15
  82.8 1.7 %copy-start.1 = (bf16[32,2,200,128]{3,2,1,0:T(8,128)(2,1)}, bf16[32,2,200,128]{3,2,1,0:T(8,128)(2,1)S(1)}, u32[]{:S(2)}) copy-start(bf16[32,2,200,128]{3,2,1,0:T(8,128)(2,1)S(1)} %fusion) | copy-start | bytes 9830404
  84.5 82.5 %all-to-all-start.1 = ((bf16[32,2,200,128]{3,2,1,0:T(8,128)(2,1)}), bf16[32,2,200,128]{3,2,1,0:T(8,128)(2,1)S(1)}, u32[]{:S(2)}, u32[]{:S(2)}) async-start(bf16[32,2,200,128]{3,2,1,0:T(8,128)(2,1)} %copy-done.1), calls=%async_computation.1 | async-start | bytes 6553600 | tf_op jit(solution)/shard_map/all_to_all | solution.py:9
